TPU v7x, 256 devices: a whole 4x4x8 slice. The times are simulated.
256 devices in a mesh: blk: 16 (over x, z_hi), slab: 16 (over y, z_lo, core).
Axes of the slice: x: 4, y: 4, z: 8 (z_hi: 4, z_lo: 2; z = z_hi * 2 + z_lo), core: 2. Of those that a mesh axis runs over, the one named last changes fastest.
Arguments:
- xinv: bfloat16 [16, 4096, 4096], P('blk', None, 'slab'), may hold values from -1 to 16
- ymat: bfloat16 [16, 4096, 4096], P('blk', None, 'slab'), may hold values from -1 to 16
- basis: bfloat16 [16, 4096, 1024], P('blk', 'slab'), may hold values from -0.08118988 to 0.08118988
- pair_index: int32 [16, 2, 512], P('blk'), may hold values from 0 to 1023
- orders: int32 [16], replicated, may hold values from 1 to 512, 4096 in all
- dest: int32 [16], replicated, may hold values from 0 to 15, each once
Outputs:
- factor: float32 [16, 512, 512], P('blk', 'slab')
Inputs may be any that keep to these rules, and one draw needn't show every extreme that they name: `pair_index`: entries name columns of the block's basis. Sum of all orders is 4096; the largest equals 512. `dest`: every group receives exactly one block.
All inputs are finite; a program needn't handle non-finite values.
Results may differ from a plain program's by a relative error of at most 0.0003.
Values may be sent and summed in bfloat16 or wider, within the bound.
A program may use at most 64 MiB of HBM per device.

v0:
```python
import jax
import jax.numpy as jnp
from jax import lax
from jax.sharding import PartitionSpec as P


def cut_along(value, dim, length):
    before, after = (value.shape[:dim], value.shape[dim + 1 :])
    return jnp.moveaxis(value.reshape(*before, length, -1, *after), dim, 0)


def sum_at_owner(value, axis, dim):
    parts = cut_along(value, dim, lax.axis_size(axis))
    arrived = lax.all_to_all(parts, axis, split_axis=0, concat_axis=0, tiled=True)
    return arrived.sum(axis=0)


def from_everyone(value, axis):
    copies = jnp.broadcast_to(value, (lax.axis_size(axis), *value.shape))
    return lax.all_to_all(copies, axis, split_axis=0, concat_axis=0, tiled=True)


def in_order(parts, dim):
    parts = jnp.moveaxis(parts, 0, dim)
    lengths = parts.shape
    return parts.reshape(*lengths[:dim], lengths[dim] * lengths[dim + 1], *lengths[dim + 2 :])


def gathered_copies(value, axis, dim):
    parts = from_everyone(value, axis)
    return in_order(parts, dim)


def add_piece(piece, columns):
    return lax.dot_general(
        piece, columns, (((0,), (0,)), ((), ())), preferred_element_type=jnp.float32
    )


def on_device(xinv, ymat, basis, pair_index, orders, dest):
    xlocal = xinv[0]
    ylocal = ymat[0]
    vlocal = basis[0]
    piece = lax.all_gather(vlocal, "slab", axis=0, tiled=True)
    cx = add_piece(piece, xlocal)
    cy = add_piece(piece, ylocal)
    cx = cx.astype(jnp.bfloat16)
    cy = cy.astype(jnp.bfloat16)
    first = pair_index[0, 0]
    second = pair_index[0, 1]
    order_most = first.shape[0]
    share = order_most // lax.axis_size("slab")
    row_start = lax.axis_index("slab") * share
    basis_first = jnp.take(vlocal, first, axis=1)
    basis_second = jnp.take(vlocal, second, axis=1)
    cx_first = jnp.take(cx, first, axis=0)
    cy_second = jnp.take(cy, second, axis=0)
    stacked = sum_at_owner(
        jnp.concatenate(
            [
                jnp.dot(cx_first, basis_first, preferred_element_type=jnp.float32),
                jnp.dot(cy_second, basis_second, preferred_element_type=jnp.float32),
            ],
            axis=1,
        ),
        "slab",
        0,
    )
    a_ff = stacked[:, :order_most]
    b_ss = stacked[:, order_most:]
    schur = a_ff * b_ss
    block_id = lax.axis_index("blk")
    order = orders[block_id]
    row_ids = row_start + jnp.arange(share, dtype=jnp.int32)
    col_ids = jnp.arange(order_most, dtype=jnp.int32)
    mask = (row_ids[:, None] < order) & (col_ids[None, :] < order)
    diagonal = (row_ids[:, None] == col_ids[None, :]).astype(jnp.float32)
    schur_rows = jnp.where(mask, schur, 0.0) + diagonal
    everyone = gathered_copies(schur_rows, "blk", 0)
    groups = dest.shape[0]
    everyone = everyone.reshape(groups, share, order_most)
    chosen = (dest == block_id).astype(jnp.float32)
    mine = jnp.sum(chosen[:, None, None] * everyone, axis=0)
    whole = gathered_copies(mine, "slab", 0)
    lower = jnp.linalg.cholesky(whole)
    own = lax.dynamic_slice_in_dim(lower, row_start, share, 0)
    return own[None]


def solution(mesh):
    return jax.shard_map(
        on_device,
        mesh=mesh,
        in_specs=(
            P("blk", None, "slab"),
            P("blk", None, "slab"),
            P("blk", "slab", None),
            P("blk", None, None),
            P(),
            P(),
        ),
        out_specs=P("blk", "slab", None),
        check_vma=False,
    )
```

profile of v0, /device:TPU:1, one launch (start us, length us, event | category | flops | bytes accessed | tf_op | source)
XLA Modules:
  0.0 283.8 jit_solution(7355366731148311306)
XLA Ops:
  6.5 0.7 all-gather.3.cloned.1.call-update
  7.3 1.2 copy.12
  8.5 0.8 fusion.46
  9.3 2.0 gather_fusion.1
  11.3 2.0 gather_fusion.3
  13.3 54.8 %all-gather.3.cloned.1.call-done = bf16[1,4096,1024]{2,1,0:T(8,128)(2,1)} async-done(((bf16[1,256,1024]{2,1,0:T(8,128)(2,1)}), bf16[1,4096,1024]{2,1,0:T(8,128)(2,1)}) %all-gather.3.cloned.1.call-update) | async-done | bytes 8388624 | tf_op jit(solution)/shard_map/all_gather | solution.py:44
  68.1 5.8 %fusion.6 = bf16[1024,256]{1,0:T(8,128)(2,1)S(1)} fusion(bf16[1,4096,256]{2,1,0:T(8,128)(2,1)S(1)} %copy-done, bf16[1,4096,1024]{2,1,0:T(8,128)(2,1)} %all-gather.3.cloned.1.call-done), kind=kOutput, calls=%fused_computation.11 | convolution fusion | flops 2147745792 | bytes 11010048 | tf_op jit(solution)/shard_map/dot_general | solution.py:35
  73.8 2.0 gather_fusion
  75.8 6.3 %fusion.11 = bf16[1024,256]{1,0:T(8,128)(2,1)S(1)} fusion(bf16[1,4096,256]{2,1,0:T(8,128)(2,1)} %param.11, bf16[1,4096,1024]{2,1,0:T(8,128)(2,1)} %all-gather.3.cloned.1.call-done), kind=kOutput, calls=%fused_computation.12 | convolution fusion | flops 2147745792 | bytes 11010048 | tf_op jit(solution)/shard_map/dot_general | solution.py:35
  82.1 2.6 gather_fusion.2
  84.7 1.4 fusion.18
  86.1 0.4 fusion.20
  86.5 1.5 pad_maximum_fusion
  88.0 2.9 %copy.13 = f32[512,1024]{1,0:T(8,128)} copy(f32[512,1024]{0,1:T(8,128)} %pad_maximum_fusion) | data formatting | bytes 4194304 | tf_op jit(solution)/shard_map/concatenate | solution.py:59
  90.9 5.3 %all-to-all-start = ((f32[16,32,1024]{2,1,0:T(8,128)}), f32[16,32,1024]{2,1,0:T(8,128)}, u32[]{:S(2)}, u32[]{:S(2)}) async-start(f32[16,32,1024]{2,1,0:T(8,128)} %bitcast.59), calls=%async_computation | async-start | bytes 4194304 | tf_op jit(solution)/shard_map/all_to_all | solution.py:14
  96.3 0.6 dynamic_slice.6
  96.9 0.6 iota_compare_fusion.4
  97.5 0.7 broadcast_compare_fusion
  98.2 25.1 %all-to-all-done = f32[16,32,1024]{2,1,0:T(8,128)} async-done(((f32[16,32,1024]{2,1,0:T(8,128)}), f32[16,32,1024]{2,1,0:T(8,128)}, u32[]{:S(2)}, u32[]{:S(2)}) %all-to-all-start) | async-done | bytes 2097184 | tf_op jit(solution)/shard_map/all_to_all | solution.py:14
  123.3 1.7 reduce_sum.18
  125.1 1.1 broadcast_in_dim.39
  126.3 8.4 %all-to-all-start.1 = ((f32[16,32,512]{2,1,0:T(8,128)}), f32[16,32,512]{2,1,0:T(8,128)S(1)}, u32[]{:S(2)}, u32[]{:S(2)}) async-start(f32[16,32,512]{2,1,0:T(8,128)} %broadcast_in_dim.39), calls=%async_computation.1 | async-start | bytes 2097152 | tf_op jit(solution)/shard_map/all_to_all | solution.py:20
  134.7 24.1 %all-to-all-done.1 = f32[16,32,512]{2,1,0:T(8,128)S(1)} async-done(((f32[16,32,512]{2,1,0:T(8,128)}), f32[16,32,512]{2,1,0:T(8,128)S(1)}, u32[]{:S(2)}, u32[]{:S(2)}) %all-to-all-start.1) | async-done | bytes 1048608 | tf_op jit(solution)/shard_map/all_to_all | solution.py:20
  158.8 0.1 multiply_reduce_fusion
  158.9 1.1 broadcast_in_dim.40
  160.1 9.9 %all-to-all-start.2 = ((f32[16,32,512]{2,1,0:T(8,128)}), f32[16,32,512]{2,1,0:T(8,128)S(1)}, u32[]{:S(2)}, u32[]{:S(2)}) async-start(f32[16,32,512]{2,1,0:T(8,128)} %broadcast_in_dim.40), calls=%async_computation.2 | async-start | bytes 2097152 | tf_op jit(solution)/shard_map/all_to_all | solution.py:20
  170.0 15.7 %all-to-all-done.2 = f32[16,32,512]{2,1,0:T(8,128)S(1)} async-done(((f32[16,32,512]{2,1,0:T(8,128)}), f32[16,32,512]{2,1,0:T(8,128)S(1)}, u32[]{:S(2)}, u32[]{:S(2)}) %all-to-all-start.2) | async-done | bytes 1048608 | tf_op jit(solution)/shard_map/all_to_all | solution.py:20
  185.6 1.3 copy.14
  187.0 1.4 fusion.16
  188.3 1.0 copy-done.1
  189.3 11.7 %cholesky.104 = f32[128,128]{1,0:T(8,128)S(1)} custom-call(f32[128,128]{1,0:T(8,128)S(1)} %cholesky.266), custom_call_target="Cholesky" | custom-call | tf_op jit(solution)/shard_map/jit(cholesky)/cholesky | solution.py:85
  201.1 0.1 cholesky.224
  201.2 9.8 %custom-call.27 = f32[1,128,128]{1,2,0:T(8,128)S(1)} custom-call(f32[1,128,128]{2,1,0:T(8,128)S(1)} %get-tuple-element.16), custom_call_target="InvertDiagBlocksLowerTriangular" | custom-call | tf_op jit(solution)/shard_map/jit(cholesky)/cholesky | solution.py:85
  211.0 1.2 constant_dynamic-update-slice_fusion.2
  212.3 1.3 convolution_subtract_fusion
  213.6 11.7 %cholesky.217 = f32[128,128]{1,0:T(8,128)S(1)} custom-call(f32[128,128]{1,0:T(8,128)S(1)} %cholesky.270), custom_call_target="Cholesky" | custom-call | tf_op jit(solution)/shard_map/jit(cholesky)/cholesky | solution.py:85
  225.3 10.0 %custom-call.28 = f32[1,128,128]{1,2,0:T(8,128)S(1)} custom-call(f32[1,128,128]{2,1,0:T(8,128)S(1)} %get-tuple-element.13), custom_call_target="InvertDiagBlocksLowerTriangular" | custom-call | tf_op jit(solution)/shard_map/jit(cholesky)/cholesky | solution.py:85
  235.3 0.3 convolution_dynamic-update-slice_fusion
  235.6 1.3 convolution_subtract_fusion.1
  236.9 11.7 %cholesky.238 = f32[128,128]{1,0:T(8,128)S(1)} custom-call(f32[128,128]{1,0:T(8,128)S(1)} %cholesky.275), custom_call_target="Cholesky" | custom-call | tf_op jit(solution)/shard_map/jit(cholesky)/cholesky | solution.py:85
  248.6 0.7 compare_reduce_fusion.1
  249.3 9.8 %custom-call.29 = f32[1,128,128]{1,2,0:T(8,128)S(1)} custom-call(f32[1,128,128]{2,1,0:T(8,128)S(1)} %get-tuple-element.10), custom_call_target="InvertDiagBlocksLowerTriangular" | custom-call | tf_op jit(solution)/shard_map/jit(cholesky)/cholesky | solution.py:85
  259.2 0.2 convolution_dynamic-update-slice_fusion.1
  259.4 1.2 convolution_subtract_fusion.2
  260.6 11.7 %cholesky.255 = f32[128,128]{1,0:T(8,128)S(1)} custom-call(f32[128,128]{1,0:T(8,128)S(1)} %convolution_subtract_fusion.2), custom_call_target="Cholesky" | custom-call | tf_op jit(solution)/shard_map/jit(cholesky)/cholesky | solution.py:85
  272.3 0.7 compare_reduce_fusion
  273.1 0.6 compare_reduce_fusion.2
  276.3 0.6 fusion.36
  (24 shorter events, 0.3 us)
Async XLA Ops:
  6.5 61.5 %copy-start = (bf16[1,4096,256]{2,1,0:T(8,128)(2,1)S(1)}, bf16[1,4096,256]{2,1,0:T(8,128)(2,1)}, u32[]{:S(2)}) copy-start(bf16[1,4096,256]{2,1,0:T(8,128)(2,1)} %param.10) | copy-start | bytes 6291460
  6.5 61.5 %all-gather.3.cloned.1.call-start = ((), (), s32[]{:S(2)}) async-start(), calls=%async_computation.3 | async-start | bytes 8912896 | tf_op jit(solution)/shard_map/all_gather | solution.py:44
  90.9 5.3 %copy-start.2 = (s32[16]{0:T(128)S(1)}, s32[16]{0:T(128)}, u32[]{:S(2)}) copy-start(s32[16]{0:T(128)} %param.14) | copy-start | bytes 196
  90.9 32.4 %all-to-all-start = ((f32[16,32,1024]{2,1,0:T(8,128)}), f32[16,32,1024]{2,1,0:T(8,128)}, u32[]{:S(2)}, u32[]{:S(2)}) async-start(f32[16,32,1024]{2,1,0:T(8,128)} %bitcast.59), calls=%async_computation | async-start | bytes 4194304 | tf_op jit(solution)/shard_map/all_to_all | solution.py:14
  125.0 9.7 %copy-start.3 = (s32[16]{0:T(128)S(1)}, s32[16]{0:T(128)}, u32[]{:S(2)}) copy-start(s32[16]{0:T(128)} %param.15) | copy-start | bytes 196
  126.3 32.5 %all-to-all-start.1 = ((f32[16,32,512]{2,1,0:T(8,128)}), f32[16,32,512]{2,1,0:T(8,128)S(1)}, u32[]{:S(2)}, u32[]{:S(2)}) async-start(f32[16,32,512]{2,1,0:T(8,128)} %broadcast_in_dim.39), calls=%async_computation.1 | async-start | bytes 2097152 | tf_op jit(solution)/shard_map/all_to_all | solution.py:20
  160.1 25.6 %all-to-all-start.2 = ((f32[16,32,512]{2,1,0:T(8,128)}), f32[16,32,512]{2,1,0:T(8,128)S(1)}, u32[]{:S(2)}, u32[]{:S(2)}) async-start(f32[16,32,512]{2,1,0:T(8,128)} %broadcast_in_dim.40), calls=%async_computation.2 | async-start | bytes 2097152 | tf_op jit(solution)/shard_map/all_to_all | solution.py:20
  188.3 1.0 copy-start.1
Sparse Core Ops, SparseCore 0:
  9.2 58.8 all-gather.2
where the time goes:
time: 284 us
  waiting for transfers between devices  120 us (42%)
  other arithmetic  85.4 us (30%)
  starting transfers between devices  23.7 us (8%)
  matrix products  19.3 us (7%)
  local copies, waits for them, and re-layouts  18.7 us (7%)
  between operations  16.3 us (6%)
    another operation x14, other arithmetic, on_device(): lower = jnp.linalg.cholesky(whole)  78.7 us
    all_gather x1, waiting for transfers between devices, on_device(): piece = lax.all_gather(vlocal, 'slab', axis=0, tiled=True)  54.8 us
    all_to_all x2, waiting for transfers between devices, from_everyone(): return lax.all_to_all(copies, axis, split_axis=0, concat_axis=0, tiled=True)  39.7 us
    all_to_all x1, waiting for transfers between devices, sum_at_owner(): lax.all_to_all(parts, axis, split_axis=0, concat_axis=0, tiled=True)  25.1 us
    all_to_all x2, starting transfers between devices, from_everyone(): return lax.all_to_all(copies, axis, split_axis=0, concat_axis=0, tiled=True)  18.4 us
    dot_general x2, matrix products, add_piece(): lax.dot_general(piece, columns, (((0,), (0,)), ((), ())), preferred_eleme...  12.1 us
  transfers between devices with their start and end apart: 4, of which 4 were waited for; matrix products, arithmetic and copies ran while one was open for 3% of the time, Pallas kernels for 0%

commit v1 on v0

--- a/solution.py
+++ b/solution.py
@@ -41,7 +41,9 @@
     xlocal = xinv[0]
     ylocal = ymat[0]
     vlocal = basis[0]
-    piece = lax.all_gather(vlocal, "slab", axis=0, tiled=True)
+    piece = jnp.concatenate(
+        lax.all_to_all(jnp.stack([vlocal] * lax.axis_size("slab")), "slab", 0, 0), axis=0
+    )
     cx = add_piece(piece, xlocal)
     cy = add_piece(piece, ylocal)
     cx = cx.astype(jnp.bfloat16)

time: 284 us -> 318 us (1.12)
  waiting for transfers between devices: 120 us -> 155 us
  between operations: 16.3 us -> 2.9 us
  starting transfers between devices: 23.7 us -> 32.4 us
  local copies, waits for them, and re-layouts: 18.7 us -> 22.4 us
    all_to_all x0 -> x1, waiting for transfers between devices: none -> 90.3 us  [on_device(): lax.all_to_all(jnp.stack([vlocal] * lax.axis_size('slab')), 'slab', 0, 0)]
    all_gather x1 -> x0, waiting for transfers between devices: 54.8 us -> none  [on_device(): piece = lax.all_gather(vlocal, 'slab', axis=0, tiled=True)]
    all_to_all x0 -> x1, starting transfers between devices: none -> 7.8 us  [on_device(): lax.all_to_all(jnp.stack([vlocal] * lax.axis_size('slab')), 'slab', 0, 0)]
    another operation x0 -> x1, local copies, waits for them, and re-layouts: none -> 5.48 us  [on_device(): jnp.stack([vlocal] * lax.axis_size('slab'))]
  transfers between devices with their start and end apart: 4 -> 4, of which waited for: 4 -> 4; matrix products, arithmetic and copies ran while one was open for 3% -> 2% of each run, Pallas kernels for 0% -> 0%
where the time goes in v1:
time: 318 us
  waiting for transfers between devices  155 us (49%)
  other arithmetic  85.4 us (27%)
  starting transfers between devices  32.4 us (10%)
  local copies, waits for them, and re-layouts  22.4 us (7%)
  matrix products  19.4 us (6%)
    all_to_all x1, waiting for transfers between devices, on_device(): lax.all_to_all(jnp.stack([vlocal] * lax.axis_size('slab')), 'slab', 0, 0)  90.3 us
    another operation x14, other arithmetic, on_device(): lower = jnp.linalg.cholesky(whole)  78.7 us
    all_to_all x2, waiting for transfers between devices, from_everyone(): return lax.all_to_all(copies, axis, split_axis=0, concat_axis=0, tiled=True)  39.7 us
    all_to_all x1, waiting for transfers between devices, sum_at_owner(): lax.all_to_all(parts, axis, split_axis=0, concat_axis=0, tiled=True)  25.2 us
    all_to_all x2, starting transfers between devices, from_everyone(): return lax.all_to_all(copies, axis, split_axis=0, concat_axis=0, tiled=True)  19.3 us
    dot_general x2, matrix products, add_piece(): lax.dot_general(piece, columns, (((0,), (0,)), ((), ())), preferred_eleme...  12.1 us
    all_to_all x1, starting transfers between devices, on_device(): lax.all_to_all(jnp.stack([vlocal] * lax.axis_size('slab')), 'slab', 0, 0)  7.8 us
  transfers between devices with their start and end apart: 4, of which 4 were waited for; matrix products, arithmetic and copies ran while one was open for 2% of the time, Pallas kernels for 0%

profile of v1, /device:TPU:1, one launch (start us, length us, event | category | flops | bytes accessed | tf_op | source)
XLA Modules:
  0.0 317.7 jit_solution(18185690546798684458)
XLA Ops:
  0.0 5.5 %stack.3 = bf16[16,256,1024]{2,1,0:T(8,128)(2,1)} broadcast(bf16[256,1024]{1,0:T(8,128)(2,1)} %bitcast.55), dimensions={1,2} | broadcast | bytes 8912896 | tf_op jit(solution)/shard_map/stack | solution.py:45
  5.5 7.8 %all-to-all-start = ((bf16[16,256,1024]{2,1,0:T(8,128)(2,1)}), bf16[16,256,1024]{2,1,0:T(8,128)(2,1)}, u32[]{:S(2)}, u32[]{:S(2)}) async-start(bf16[16,256,1024]{2,1,0:T(8,128)(2,1)} %stack.3), calls=%async_computation | async-start | bytes 16777216 | tf_op jit(solution)/shard_map/all_to_all | solution.py:45
  13.3 0.2 copy.14
  13.5 2.0 gather_fusion.1
  15.5 2.0 gather_fusion.3
  17.5 90.3 %all-to-all-done = bf16[16,256,1024]{2,1,0:T(8,128)(2,1)} async-done(((bf16[16,256,1024]{2,1,0:T(8,128)(2,1)}), bf16[16,256,1024]{2,1,0:T(8,128)(2,1)}, u32[]{:S(2)}, u32[]{:S(2)}) %all-to-all-start) | async-done | bytes 8388640 | tf_op jit(solution)/shard_map/all_to_all | solution.py:45
  107.8 5.8 %fusion.4 = bf16[1024,256]{1,0:T(8,128)(2,1)S(1)} fusion(bf16[4096,1024]{1,0:T(8,128)(2,1)} %bitcast.4, bf16[1,4096,256]{2,1,0:T(8,128)(2,1)S(1)} %copy-done), kind=kOutput, calls=%fused_computation.9 | convolution fusion | flops 2147745792 | bytes 11010048 | tf_op jit(solution)/shard_map/dot_general | solution.py:35
  113.6 2.0 gather_fusion
  115.6 6.4 %fusion.7 = bf16[1024,256]{1,0:T(8,128)(2,1)S(1)} fusion(bf16[4096,1024]{1,0:T(8,128)(2,1)} %bitcast.4, bf16[1,4096,256]{2,1,0:T(8,128)(2,1)} %param.11), kind=kOutput, calls=%fused_computation.10 | convolution fusion | flops 2147745792 | bytes 11010048 | tf_op jit(solution)/shard_map/dot_general | solution.py:35
  121.9 2.6 gather_fusion.2
  124.5 0.4 fusion.14
  124.9 1.4 fusion.12
  126.3 1.5 pad_maximum_fusion
  127.8 2.9 copy.16
  130.7 5.3 %all-to-all-start.1 = ((f32[16,32,1024]{2,1,0:T(8,128)}), f32[16,32,1024]{2,1,0:T(8,128)}, u32[]{:S(2)}, u32[]{:S(2)}) async-start(f32[16,32,1024]{2,1,0:T(8,128)} %bitcast.54), calls=%async_computation.1 | async-start | bytes 4194304 | tf_op jit(solution)/shard_map/all_to_all | solution.py:14
  136.0 0.6 dynamic_slice.6
  136.6 0.6 iota_compare_fusion.4
  137.2 0.7 broadcast_compare_fusion
  137.9 25.2 %all-to-all-done.1 = f32[16,32,1024]{2,1,0:T(8,128)} async-done(((f32[16,32,1024]{2,1,0:T(8,128)}), f32[16,32,1024]{2,1,0:T(8,128)}, u32[]{:S(2)}, u32[]{:S(2)}) %all-to-all-start.1) | async-done | bytes 2097184 | tf_op jit(solution)/shard_map/all_to_all | solution.py:14
  163.1 1.7 reduce_sum.18
  164.9 1.1 broadcast_in_dim.39
  166.1 9.4 %all-to-all-start.2 = ((f32[16,32,512]{2,1,0:T(8,128)}), f32[16,32,512]{2,1,0:T(8,128)S(1)}, u32[]{:S(2)}, u32[]{:S(2)}) async-start(f32[16,32,512]{2,1,0:T(8,128)} %broadcast_in_dim.39), calls=%async_computation.2 | async-start | bytes 2097152 | tf_op jit(solution)/shard_map/all_to_all | solution.py:20
  175.5 24.1 %all-to-all-done.2 = f32[16,32,512]{2,1,0:T(8,128)S(1)} async-done(((f32[16,32,512]{2,1,0:T(8,128)}), f32[16,32,512]{2,1,0:T(8,128)S(1)}, u32[]{:S(2)}, u32[]{:S(2)}) %all-to-all-start.2) | async-done | bytes 1048608 | tf_op jit(solution)/shard_map/all_to_all | solution.py:20
  199.6 0.1 multiply_reduce_fusion
  199.7 1.1 broadcast_in_dim.40
  200.8 9.9 %all-to-all-start.3 = ((f32[16,32,512]{2,1,0:T(8,128)}), f32[16,32,512]{2,1,0:T(8,128)S(1)}, u32[]{:S(2)}, u32[]{:S(2)}) async-start(f32[16,32,512]{2,1,0:T(8,128)} %broadcast_in_dim.40), calls=%async_computation.3 | async-start | bytes 2097152 | tf_op jit(solution)/shard_map/all_to_all | solution.py:20
  210.8 15.7 %all-to-all-done.3 = f32[16,32,512]{2,1,0:T(8,128)S(1)} async-done(((f32[16,32,512]{2,1,0:T(8,128)}), f32[16,32,512]{2,1,0:T(8,128)S(1)}, u32[]{:S(2)}, u32[]{:S(2)}) %all-to-all-start.3) | async-done | bytes 1048608 | tf_op jit(solution)/shard_map/all_to_all | solution.py:20
  226.4 1.3 copy.17
  227.8 1.4 fusion.10
  229.1 1.0 copy-done.1
  230.1 11.7 %cholesky.104 = f32[128,128]{1,0:T(8,128)S(1)} custom-call(f32[128,128]{1,0:T(8,128)S(1)} %cholesky.266), custom_call_target="Cholesky" | custom-call | tf_op jit(solution)/shard_map/jit(cholesky)/cholesky | solution.py:87
  241.8 0.1 cholesky.224
  242.0 9.8 %custom-call.27 = f32[1,128,128]{1,2,0:T(8,128)S(1)} custom-call(f32[1,128,128]{2,1,0:T(8,128)S(1)} %get-tuple-element.16), custom_call_target="InvertDiagBlocksLowerTriangular" | custom-call | tf_op jit(solution)/shard_map/jit(cholesky)/cholesky | solution.py:87
  251.8 1.2 constant_dynamic-update-slice_fusion.2
  253.1 1.3 convolution_subtract_fusion
  254.3 11.7 %cholesky.217 = f32[128,128]{1,0:T(8,128)S(1)} custom-call(f32[128,128]{1,0:T(8,128)S(1)} %cholesky.270), custom_call_target="Cholesky" | custom-call | tf_op jit(solution)/shard_map/jit(cholesky)/cholesky | solution.py:87
  266.1 10.0 %custom-call.28 = f32[1,128,128]{1,2,0:T(8,128)S(1)} custom-call(f32[1,128,128]{2,1,0:T(8,128)S(1)} %get-tuple-element.13), custom_call_target="InvertDiagBlocksLowerTriangular" | custom-call | tf_op jit(solution)/shard_map/jit(cholesky)/cholesky | solution.py:87
  276.1 0.3 convolution_dynamic-update-slice_fusion
  276.4 1.3 convolution_subtract_fusion.1
  277.7 11.7 %cholesky.238 = f32[128,128]{1,0:T(8,128)S(1)} custom-call(f32[128,128]{1,0:T(8,128)S(1)} %cholesky.275), custom_call_target="Cholesky" | custom-call | tf_op jit(solution)/shard_map/jit(cholesky)/cholesky | solution.py:87
  289.4 0.7 compare_reduce_fusion.1
  290.1 9.8 %custom-call.29 = f32[1,128,128]{1,2,0:T(8,128)S(1)} custom-call(f32[1,128,128]{2,1,0:T(8,128)S(1)} %get-tuple-element.10), custom_call_target="InvertDiagBlocksLowerTriangular" | custom-call | tf_op jit(solution)/shard_map/jit(cholesky)/cholesky | solution.py:87
  299.9 0.2 convolution_dynamic-update-slice_fusion.1
  300.2 1.2 convolution_subtract_fusion.2
  301.4 11.7 %cholesky.255 = f32[128,128]{1,0:T(8,128)S(1)} custom-call(f32[128,128]{1,0:T(8,128)S(1)} %convolution_subtract_fusion.2), custom_call_target="Cholesky" | custom-call | tf_op jit(solution)/shard_map/jit(cholesky)/cholesky | solution.py:87
  313.1 0.7 compare_reduce_fusion
  313.9 0.6 compare_reduce_fusion.2
  317.1 0.6 fusion.30
  (28 shorter events, 0.3 us)
Async XLA Ops:
  0.0 107.8 %copy-start = (bf16[1,4096,256]{2,1,0:T(8,128)(2,1)S(1)}, bf16[1,4096,256]{2,1,0:T(8,128)(2,1)}, u32[]{:S(2)}) copy-start(bf16[1,4096,256]{2,1,0:T(8,128)(2,1)} %param.10) | copy-start | bytes 6291460
  5.5 7.8 %copy-start.2 = (bf16[1,256,1024]{2,1,0:T(8,128)(2,1)S(1)}, bf16[1,256,1024]{2,1,0:T(8,128)(2,1)}, u32[]{:S(2)}) copy-start(bf16[1,256,1024]{2,1,0:T(8,128)(2,1)} %param.12) | copy-start | bytes 1572868
  5.5 8.0 %copy-start.3 = (s32[1,2,512]{2,1,0:T(2,128)S(1)}, s32[1,2,512]{2,1,0:T(2,128)}, u32[]{:S(2)}) copy-start(s32[1,2,512]{2,1,0:T(2,128)} %param.13) | copy-start | bytes 12292
  5.5 102.4 %all-to-all-start = ((bf16[16,256,1024]{2,1,0:T(8,128)(2,1)}), bf16[16,256,1024]{2,1,0:T(8,128)(2,1)}, u32[]{:S(2)}, u32[]{:S(2)}) async-start(bf16[16,256,1024]{2,1,0:T(8,128)(2,1)} %stack.3), calls=%async_computation | async-start | bytes 16777216 | tf_op jit(solution)/shard_map/all_to_all | solution.py:45
  130.7 5.3 %copy-start.4 = (s32[16]{0:T(128)S(1)}, s32[16]{0:T(128)}, u32[]{:S(2)}) copy-start(s32[16]{0:T(128)} %param.14) | copy-start | bytes 196
  130.7 32.4 %all-to-all-start.1 = ((f32[16,32,1024]{2,1,0:T(8,128)}), f32[16,32,1024]{2,1,0:T(8,128)}, u32[]{:S(2)}, u32[]{:S(2)}) async-start(f32[16,32,1024]{2,1,0:T(8,128)} %bitcast.54), calls=%async_computation.1 | async-start | bytes 4194304 | tf_op jit(solution)/shard_map/all_to_all | solution.py:14
  164.8 10.7 %copy-start.5 = (s32[16]{0:T(128)S(1)}, s32[16]{0:T(128)}, u32[]{:S(2)}) copy-start(s32[16]{0:T(128)} %param.15) | copy-start | bytes 196
  166.1 33.5 %all-to-all-start.2 = ((f32[16,32,512]{2,1,0:T(8,128)}), f32[16,32,512]{2,1,0:T(8,128)S(1)}, u32[]{:S(2)}, u32[]{:S(2)}) async-start(f32[16,32,512]{2,1,0:T(8,128)} %broadcast_in_dim.39), calls=%async_computation.2 | async-start | bytes 2097152 | tf_op jit(solution)/shard_map/all_to_all | solution.py:20
  200.8 25.6 %all-to-all-start.3 = ((f32[16,32,512]{2,1,0:T(8,128)}), f32[16,32,512]{2,1,0:T(8,128)S(1)}, u32[]{:S(2)}, u32[]{:S(2)}) async-start(f32[16,32,512]{2,1,0:T(8,128)} %broadcast_in_dim.40), calls=%async_computation.3 | async-start | bytes 2097152 | tf_op jit(solution)/shard_map/all_to_all | solution.py:20
  229.1 1.0 copy-start.1
